TPU v7x, 32 devices: a whole 2x2x4 slice. The times are simulated.
32 devices in a mesh: coil: 4 (over x, core), slab: 8 (over z, y).
Axes of the slice: x: 2, y: 2, z: 4, core: 2. Of those that a mesh axis runs over, the one named last changes fastest.
Arguments:
- kspace_data: bfloat16 [32, 2, 128, 128, 128], P('coil', None, None, 'slab'), may hold values from -4 to 4
- coil_maps: bfloat16 [32, 2, 128, 128, 128], P('coil', None, 'slab'), may hold values from -1.796875 to 1.796875
- sample_mask: int32 [32, 128, 128], P('coil', None, 'slab'), may hold values 0 or 1
- initial_image: float32 [2, 128, 128, 128], P(None, 'slab', 'coil'), may hold values from -6 to 6
Outputs:
- image: float32 [2, 128, 128, 128], P(None, 'slab', 'coil')
All inputs are finite; a program needn't handle non-finite values. No bound on the sum of `sample_mask` on one device may be relied on, other than what follows from the above.
Results may differ from a plain program's by a relative error of at most 0.0045.
Values may be sent and summed in bfloat16 or wider, within the bound.
A program may use at most 128 MiB of HBM per device.

v0:
```python
import math
import jax
import jax.numpy as jnp
from jax import lax
from jax.sharding import PartitionSpec as P

NX = 128
NY = 128
NZ = 128
ITERS = 2
dual_step = 0.25
primal_step = 0.25
tv_weight = 0.5


def from_behind(block, axis, distance):
    devices = range(lax.axis_size(axis))
    route = [(i - distance, i) for i in devices if i - distance in devices]
    return lax.ppermute(block, axis, route)


def dft_table(length, inverse):
    counter = jnp.arange(length, dtype=jnp.int32)
    product = counter[:, None] * counter[None, :] % length
    phase = 2.0 * math.pi / length * product.astype(jnp.float32)
    scale = 1.0 / math.sqrt(length)
    real_part = jnp.cos(phase) * scale
    imag_part = jnp.sin(phase) * scale
    if not inverse:
        imag_part = -imag_part
    table = jnp.stack([jnp.stack([real_part, imag_part]), jnp.stack([-imag_part, real_part])])
    return table.astype(jnp.bfloat16)


def data_term(guess, coil_maps, kspace_data, sample_mask, dual_data, tables):
    forward_x, forward_y, forward_z, inverse_x, inverse_y, inverse_z = tables
    maps_real = coil_maps[:, 0].astype(jnp.float32)
    maps_imag = coil_maps[:, 1].astype(jnp.float32)
    pieces = jnp.stack(
        [maps_real * guess[0] - maps_imag * guess[1], maps_real * guess[1] + maps_imag * guess[0]],
        1,
    ).astype(jnp.bfloat16)
    pieces = jnp.einsum(
        "ckzyx,kjxw->cjzyw", pieces, forward_x, preferred_element_type=jnp.float32
    ).astype(jnp.bfloat16)
    pieces = jnp.einsum(
        "ckzyx,kjyv->cjzvx", pieces, forward_y, preferred_element_type=jnp.float32
    ).astype(jnp.bfloat16)
    spectrum = jnp.einsum(
        "ckzyx,kjzw->cjwyx",
        lax.all_to_all(pieces, "slab", split_axis=3, concat_axis=2, tiled=True),
        forward_z,
        preferred_element_type=jnp.float32,
    )
    sampled = sample_mask[:, None, :, :, None].astype(jnp.float32)
    dual_new = (
        dual_data + dual_step * (sampled * (spectrum - kspace_data.astype(jnp.float32)))
    ) / (1.0 + dual_step)
    back_field = jnp.einsum(
        "ckzyx,kjzw->cjwyx",
        dual_new.astype(jnp.bfloat16),
        inverse_z,
        preferred_element_type=jnp.float32,
    ).astype(jnp.bfloat16)
    back_field = jnp.einsum(
        "ckzyx,kjyv->cjzvx",
        lax.all_to_all(back_field, "slab", split_axis=2, concat_axis=3, tiled=True),
        inverse_y,
        preferred_element_type=jnp.float32,
    ).astype(jnp.bfloat16)
    back_field = jnp.einsum(
        "ckzyx,kjxw->cjzyw", back_field, inverse_x, preferred_element_type=jnp.float32
    )
    real_sum = jnp.sum(maps_real * back_field[:, 0] + maps_imag * back_field[:, 1], 0)
    imag_sum = jnp.sum(maps_real * back_field[:, 1] - maps_imag * back_field[:, 0], 0)
    return (jnp.stack([real_sum, imag_sum]), dual_new)


def tv_update(guess, duals):
    planes = guess.shape[1]
    plane_pos = lax.axis_index("slab") * planes + lax.broadcasted_iota(
        jnp.int32, (1, planes, 1, 1), 1
    )
    next_plane = from_behind(guess[:, :1], "slab", -1)
    ahead_z = jnp.concatenate([guess[:, 1:], next_plane], 1)
    grad_z = jnp.where(plane_pos < NZ - 1, ahead_z - guess, 0.0)
    grad_y = jnp.concatenate(
        [guess[:, :, 1:] - guess[:, :, :-1], jnp.zeros_like(guess[:, :, :1])], 2
    )
    grad_x = jnp.concatenate([guess[..., 1:] - guess[..., :-1], jnp.zeros_like(guess[..., :1])], 3)
    moved_z = duals[0] + dual_step * grad_z
    moved_y = duals[1] + dual_step * grad_y
    moved_x = duals[2] + dual_step * grad_x
    magnitude = jnp.sqrt(
        jnp.sum(moved_z * moved_z, 0)
        + jnp.sum(moved_y * moved_y, 0)
        + jnp.sum(moved_x * moved_x, 0)
    )
    factor = 1.0 / jnp.maximum(1.0, magnitude / tv_weight)
    dual_z = moved_z * factor
    dual_y = moved_y * factor
    dual_x = moved_x * factor
    prior_plane = from_behind(dual_z[:, -1:], "slab", 1)
    spread_z = jnp.concatenate([prior_plane, dual_z[:, :-1]], 1) - dual_z
    spread_y = jnp.concatenate([jnp.zeros_like(dual_y[:, :, :1]), dual_y[:, :, :-1]], 2) - dual_y
    spread_x = jnp.concatenate([jnp.zeros_like(dual_x[..., :1]), dual_x[..., :-1]], 3) - dual_x
    return ((dual_z, dual_y, dual_x), spread_z + spread_y + spread_x)


def on_device(kspace_data, coil_maps, sample_mask, initial_image):
    tables = (
        dft_table(NX, False),
        dft_table(NY, False),
        dft_table(NZ, False),
        dft_table(NX, True),
        dft_table(NY, True),
        dft_table(NZ, True),
    )
    dual_data = jnp.zeros(kspace_data.shape, jnp.float32)
    share_rows = initial_image.shape[2]
    current = initial_image
    guess = current
    duals = None
    for turn_index in range(ITERS):
        whole_guess = lax.all_gather(guess, "coil", axis=2, tiled=True)
        if duals is None:
            duals = (
                jnp.zeros_like(whole_guess),
                jnp.zeros_like(whole_guess),
                jnp.zeros_like(whole_guess),
            )
        data_grad, dual_data = data_term(
            whole_guess, coil_maps, kspace_data, sample_mask, dual_data, tables
        )
        data_grad = lax.psum_scatter(data_grad, "coil", scatter_dimension=2, tiled=True)
        duals, spread = tv_update(whole_guess, duals)
        spread_share = lax.dynamic_slice_in_dim(
            spread, lax.axis_index("coil") * share_rows, share_rows, 2
        )
        updated = current - primal_step * (data_grad + spread_share)
        guess = 2.0 * updated - current
        current = updated
    return current


def solution(mesh):
    placed = (
        P("coil", None, None, "slab", None),
        P("coil", None, "slab", None, None),
        P("coil", None, "slab"),
        P(None, "slab", "coil", None),
    )
    return jax.shard_map(
        on_device,
        mesh=mesh,
        in_specs=placed,
        out_specs=P(None, "slab", "coil", None),
        check_vma=False,
    )
```

profile of v0, /device:TPU:0, one launch (start us, length us, event | category | flops | bytes accessed | tf_op | source)
XLA Modules:
  0.0 1111.8 jit_solution(6184151116436738106)
XLA Ops:
  9.3 24.9 %all-gather.3.cloned.1.call-done = f32[2,16,128,128]{3,1,0,2:T(8,128)} async-done(((f32[2,16,32,128]{3,1,0,2:T(8,128)}), f32[2,16,128,128]{3,1,0,2:T(8,128)}) %all-gather.3.cloned.1.call-update) | async-done | bytes 2097168 | tf_op jit(solution)/shard_map/all_gather | solution.py:125
  43.0 9.0 fusion.8
  52.0 12.0 %copy.123 = bf16[8,2,16,128,128]{4,2,0,1,3:T(8,128)(2,1)} copy(bf16[8,2,16,128,128]{4,3,2,0,1:T(8,128)(2,1)} %fusion.8) | data formatting | bytes 16777216 | tf_op jit(solution)/shard_map/convert_element_type | solution.py:48
  69.9 183.3 %all-to-all-done = bf16[8,2,16,128,128]{4,2,0,1,3:T(8,128)(2,1)} async-done(((bf16[8,2,16,128,128]{4,2,0,1,3:T(8,128)(2,1)}), bf16[8,2,16,128,128]{4,2,0,1,3:T(8,128)(2,1)}, u32[]{:S(2)}, u32[]{:S(2)}) %all-to-all-start) | async-done | bytes 8388640 | tf_op jit(solution)/shard_map/all_to_all | solution.py:51
  253.2 9.1 copy.124
  262.3 12.3 %fusion.7 = (bf16[8,2,128,16,128]{4,2,3,0,1:T(8,128)(2,1)S(1)}, f32[2,128,8,16,128,1]{4,1,5,3,2,0:T(8,128)}) fusion(f32[8,128,16]{1,2,0:T(8,128)S(1)} %convert_element_type.129, bf16[8,2,128,16,128]{4,3,2,1,0:T(8,128)(2,1)} %param.4, bf16[8,2,128,16,128,1]{4,2,1,3,0,5:T(8,128)(2,1)} %bitcast.269, bf16[1,2,128,128]{2,3,0,1:T(8,128)(2,1)S(1)} %get-tuple-element.28, ...), kind=kOutput, calls=%fused_computation.33 | convolution fusion | flops 2168717312 | bytes 42139648 | tf_op jit(solution)/shard_map/ckzyx,kjzw->cjwyx/dot_general | solution.py:49
  279.1 12.0 %copy.128 = bf16[8,2,128,16,128]{4,3,0,1,2:T(8,128)(2,1)} copy(bf16[8,2,128,16,128]{4,2,3,0,1:T(8,128)(2,1)} %fusion.9) | data formatting | bytes 16777216 | tf_op jit(solution)/shard_map/convert_element_type | solution.py:64
  291.1 189.0 %all_to_all.72 = bf16[8,2,128,16,128]{4,3,0,1,2:T(8,128)(2,1)} all-to-all(bf16[8,2,128,16,128]{4,3,0,1,2:T(8,128)(2,1)} %copy.128), channel_id=1, replica_groups=mesh['coil'=4,'slab'=8] {'slab'}, dimensions={2} | all-to-all | bytes 16777216 | tf_op jit(solution)/shard_map/all_to_all | solution.py:67
  480.2 9.1 copy.130
  489.3 10.3 convolution_bitcast_fusion.1
  499.5 10.0 fusion.17
  535.5 8.4 reduce-scatter.3.cloned.1.call-done
  547.2 22.7 %all-gather.5.cloned.1.call-done = f32[2,16,128,128]{3,1,0,2:T(8,128)} async-done(((f32[2,16,32,128]{3,1,0,2:T(8,128)}), f32[2,16,128,128]{3,1,0,2:T(8,128)}) %all-gather.5.cloned.1.call-update) | async-done | bytes 2097168 | tf_op jit(solution)/shard_map/all_gather | solution.py:125
  580.5 9.0 fusion.10
  589.5 12.0 %copy.143 = bf16[8,2,16,128,128]{4,2,0,1,3:T(8,128)(2,1)} copy(bf16[8,2,16,128,128]{4,3,2,0,1:T(8,128)(2,1)} %fusion.10) | data formatting | bytes 16777216 | tf_op jit(solution)/shard_map/convert_element_type | solution.py:48
  601.5 189.6 %all_to_all.73 = bf16[8,2,16,128,128]{4,2,0,1,3:T(8,128)(2,1)} all-to-all(bf16[8,2,16,128,128]{4,2,0,1,3:T(8,128)(2,1)} %copy.143), channel_id=1, replica_groups=mesh['coil'=4,'slab'=8] {'slab'}, dimensions={3} | all-to-all | bytes 16777216 | tf_op jit(solution)/shard_map/all_to_all | solution.py:51
  791.0 16.3 %copy.145 = bf16[8,2,8,16,16,128]{5,4,3,2,1,0:T(8,128)(2,1)} copy(bf16[8,2,8,16,16,128]{5,3,0,1,4,2:T(8,128)(2,1)} %bitcast.273) | data formatting | bytes 16777216 | tf_op jit(solution)/shard_map/all_to_all | solution.py:51
  807.3 21.2 %fusion.6 = bf16[8,2,128,16,128]{4,2,3,0,1:T(8,128)(2,1)} fusion(f32[2,128,8,16,128,1]{4,1,5,3,2,0:T(8,128)} %get-tuple-element.34, f32[8,128,16]{1,2,0:T(8,128)S(1)} %convert_element_type.129, bf16[8,2,128,16,128]{4,3,2,1,0:T(8,128)(2,1)} %param.4, bf16[8,2,128,16,128]{4,3,2,1,0:T(8,128)(2,1)} %bitcast.278, ...), kind=kOutput, calls=%fused_computation.24 | convolution fusion | flops 2189688832 | bytes 42139648 | tf_op jit(solution)/shard_map/ckzyx,kjzw->cjwyx/dot_general | solution.py:49
  836.5 12.0 %copy.149 = bf16[8,2,128,16,128]{4,3,0,1,2:T(8,128)(2,1)} copy(bf16[8,2,128,16,128]{4,2,3,0,1:T(8,128)(2,1)} %fusion.11) | data formatting | bytes 16777216 | tf_op jit(solution)/shard_map/convert_element_type | solution.py:64
  848.5 188.8 %all_to_all.74 = bf16[8,2,128,16,128]{4,3,0,1,2:T(8,128)(2,1)} all-to-all(bf16[8,2,128,16,128]{4,3,0,1,2:T(8,128)(2,1)} %copy.149), channel_id=1, replica_groups=mesh['coil'=4,'slab'=8] {'slab'}, dimensions={2} | all-to-all | bytes 16777216 | tf_op jit(solution)/shard_map/all_to_all | solution.py:67
  1037.3 9.1 copy.151
  1046.4 10.3 convolution_bitcast_fusion
  1056.7 10.0 fusion.25
  1090.6 10.9 reduce-scatter.5.cloned.1.call-done
  (89 shorter events, 96.5 us)
Async XLA Ops:
  6.5 27.7 %all-gather.3.cloned.1.call-start = ((), (), s32[]{:S(2)}) async-start(), calls=%async_computation.6 | async-start | bytes 2621440 | tf_op jit(solution)/shard_map/all_gather | solution.py:125
  34.2 4.0 copy-start.1
  64.0 5.9 copy-start.11
  64.0 189.2 %all-to-all-start = ((bf16[8,2,16,128,128]{4,2,0,1,3:T(8,128)(2,1)}), bf16[8,2,16,128,128]{4,2,0,1,3:T(8,128)(2,1)}, u32[]{:S(2)}, u32[]{:S(2)}) async-start(bf16[8,2,16,128,128]{4,2,0,1,3:T(8,128)(2,1)} %copy.123), calls=%async_computation | async-start | bytes 16777216 | tf_op jit(solution)/shard_map/all_to_all | solution.py:51
  69.6 474.3 %reduce-scatter.3.cloned.1.call-start = ((), (), s32[]{:S(2)}) async-start(), calls=%async_computation.7 | async-start | bytes 2621440 | tf_op jit(solution)/shard_map/reduce_scatter | solution.py:135
  511.6 3.4 copy-start
  515.0 54.9 %all-gather.5.cloned.1.call-start = ((), (), s32[]{:S(2)}) async-start(), calls=%async_computation.8 | async-start | bytes 2621440 | tf_op jit(solution)/shard_map/all_gather | solution.py:125
  515.2 6.9 collective-permute-start
  526.5 1.3 copy-start.6
  526.5 17.4 %copy-start.3 = (f32[2,16,128,128]{3,1,0,2:T(8,128)S(1)}, f32[2,16,128,128]{3,1,0,2:T(8,128)}, u32[]{:S(2)}) copy-start(f32[2,16,128,128]{3,1,0,2:T(8,128)} %get-tuple-element.26) | copy-start | bytes 6291460
  526.5 17.4 %copy-start.10 = (f32[2,16,32,128]{3,2,1,0:T(8,128)S(1)}, f32[2,16,32,128]{3,2,1,0:T(8,128)}, u32[]{:S(2)}) copy-start(f32[2,16,32,128]{3,2,1,0:T(8,128)} %param.7) | copy-start | bytes 1572868
  528.0 7.5 collective-permute-start.1
  547.2 554.4 %reduce-scatter.5.cloned.1.call-start = ((), (), s32[]{:S(2)}) async-start(), calls=%async_computation.9 | async-start | bytes 2621440 | tf_op jit(solution)/shard_map/reduce_scatter | solution.py:135
  1068.8 3.3 copy-start.2
  1072.3 6.9 collective-permute-start.2
  1074.1 1.6 copy-start.4
  1076.3 1.8 copy-start.5
  1076.3 2.8 copy-start.7
  1083.3 4.9 copy-start.8
  1083.3 18.3 %copy-start.9 = (f32[2,16,32,128]{3,1,0,2:T(8,128)S(1)}, f32[2,16,32,128]{3,1,0,2:T(8,128)}, u32[]{:S(2)}) copy-start(f32[2,16,32,128]{3,1,0,2:T(8,128)} %get-tuple-element.12) | copy-start | bytes 1572868
  1083.4 7.2 collective-permute-start.3
Sparse Core Ops, SparseCore 0:
  8.9 25.2 all-gather.2
  515.1 28.8 reduce-scatter.2
  547.3 22.5 all-gather.4
  1072.3 29.2 reduce-scatter.4
where the time goes:
time: 1120 us; the launch traced here: 1110 us
  blocking collectives  567 us (51%)
  waiting for transfers between devices  255 us (23%)
  local copies, waits for them, and re-layouts  119 us (11%)
  matrix products  84.5 us (8%)
  other arithmetic  53.8 us (5%)
  starting transfers between devices  18 us (2%)
  between operations  14 us (1%)
    all_to_all x2, blocking collectives, data_term(): lax.all_to_all(back_field, 'slab', split_axis=2, concat_axis=3, tiled=True)  378 us
    all_to_all x1, blocking collectives, data_term(): lax.all_to_all(pieces, 'slab', split_axis=3, concat_axis=2, tiled=True)  190 us
    all_to_all x1, waiting for transfers between devices, data_term(): lax.all_to_all(pieces, 'slab', split_axis=3, concat_axis=2, tiled=True)  183 us
    all_gather x2, waiting for transfers between devices, on_device(): whole_guess = lax.all_gather(guess, 'coil', axis=2, tiled=True)  47.6 us
    dot_general x2, matrix products, data_term(): jnp.einsum('ckzyx,kjzw->cjwyx', lax.all_to_all(pieces, 'slab', split_axis...  33.5 us
    all_to_all x2, local copies, waits for them, and re-layouts, data_term(): lax.all_to_all(pieces, 'slab', split_axis=3, concat_axis=2, tiled=True)  25.4 us
    convert_element_type x2, local copies, waits for them, and re-layouts, data_term(): back_field = jnp.einsum('ckzyx,kjzw->cjwyx', dual_new.astype(jnp.bfloat16...  24 us
    convert_element_type x2, local copies, waits for them, and re-layouts, data_term(): pieces = jnp.einsum('ckzyx,kjyv->cjzvx', pieces, forward_y, preferred_ele...  24 us
  transfers between devices with their start and end apart: 9, of which 8 were waited for; matrix products, arithmetic and copies ran while one was open for 2% of the time, Pallas kernels for 0%

commit v1 on v0

--- a/solution.py
+++ b/solution.py
@@ -3,6 +3,7 @@
 import jax.numpy as jnp
 from jax import lax
 from jax.sharding import PartitionSpec as P
+from jax.lax import all_to_all, axis_size
 
 NX = 128
 NY = 128
@@ -11,6 +12,15 @@
 dual_step = 0.25
 primal_step = 0.25
 tv_weight = 0.5
+change_the_space = lambda axis_k, array_here, pos_dim, comm_axis: jnp.concatenate(
+    all_to_all(
+        jnp.stack(jnp.split(array_here, axis_size(comm_axis), axis=pos_dim)),
+        axis_name=comm_axis,
+        split_axis=0,
+        concat_axis=0,
+    ),
+    axis=axis_k,
+)
 
 
 def from_behind(block, axis, distance):
@@ -48,7 +58,7 @@
     ).astype(jnp.bfloat16)
     spectrum = jnp.einsum(
         "ckzyx,kjzw->cjwyx",
-        lax.all_to_all(pieces, "slab", split_axis=3, concat_axis=2, tiled=True),
+        change_the_space(2, array_here=pieces, pos_dim=3, comm_axis="slab"),
         forward_z,
         preferred_element_type=jnp.float32,
     )

time: 1120 us -> 1140 us (1.018)
    unnamed x29 -> x41, local copies, waits for them, and re-layouts: 8.87 us -> 42.1 us
    all_to_all x2 -> x0, local copies, waits for them, and re-layouts: 25.4 us -> none  [data_term(): lax.all_to_all(pieces, 'slab', split_axis=3, concat_axis=2, tiled=True)]
    convert_element_type x2 -> x0, local copies, waits for them, and re-layouts: 24 us -> none  [data_term(): pieces = jnp.einsum('ckzyx,kjyv->cjzvx', pieces, forward_y, preferred_ele...]
    reshape x0 -> x2, local copies, waits for them, and re-layouts: none -> 19.5 us  [jnp.concatenate(all_to_all(jnp.stack(jnp.split(array_here, axis_size(comm...]
  transfers between devices with their start and end apart: 9 -> 9, of which waited for: 8 -> 9; matrix products, arithmetic and copies ran while one was open for 2% -> 2% of each run, Pallas kernels for 0% -> 0%
where the time goes in v1:
time: 1140 us; the launch traced here: 1130 us
  blocking collectives  567 us (50%)
  waiting for transfers between devices  259 us (23%)
  local copies, waits for them, and re-layouts  124 us (11%)
  matrix products  91.8 us (8%)
  other arithmetic  59.3 us (5%)
  starting transfers between devices  17.3 us (2%)
  between operations  14 us (1%)
    all_to_all x2, blocking collectives, data_term(): lax.all_to_all(back_field, 'slab', split_axis=2, concat_axis=3, tiled=True)  378 us
    all_to_all x1, blocking collectives, all_to_all(jnp.stack(jnp.split(array_here, axis_size(comm_axis), axis=pos...  189 us
    all_to_all x1, waiting for transfers between devices, all_to_all(jnp.stack(jnp.split(array_here, axis_size(comm_axis), axis=pos...  183 us
    all_gather x2, waiting for transfers between devices, on_device(): whole_guess = lax.all_gather(guess, 'coil', axis=2, tiled=True)  47.6 us
    unnamed x41, local copies, waits for them, and re-layouts  42.1 us
    dot_general x2, matrix products, data_term(): jnp.einsum('ckzyx,kjzw->cjwyx', change_the_space(2, array_here=pieces, po...  37.2 us
    convert_element_type x2, local copies, waits for them, and re-layouts, data_term(): back_field = jnp.einsum('ckzyx,kjzw->cjwyx', dual_new.astype(jnp.bfloat16...  24 us
  transfers between devices with their start and end apart: 9, of which 9 were waited for; matrix products, arithmetic and copies ran while one was open for 2% of the time, Pallas kernels for 0%

profile of v1, /device:TPU:0, one launch (start us, length us, event | category | flops | bytes accessed | tf_op | source)
XLA Modules:
  0.0 1132.6 jit_solution(1329772320350368935)
XLA Ops:
  9.3 24.9 %all-gather.3.cloned.1.call-done = f32[2,16,128,128]{3,1,0,2:T(8,128)} async-done(((f32[2,16,32,128]{3,1,0,2:T(8,128)}), f32[2,16,128,128]{3,1,0,2:T(8,128)}) %all-gather.3.cloned.1.call-update) | async-done | bytes 2097168 | tf_op jit(solution)/shard_map/all_gather | solution.py:135
  42.9 9.0 fusion.8
  77.5 183.5 %all-to-all-done = bf16[8,8,2,16,16,128]{5,4,3,1,2,0:T(8,128)(2,1)} async-done(((bf16[8,8,2,16,16,128]{5,4,3,1,2,0:T(8,128)(2,1)}), bf16[8,8,2,16,16,128]{5,4,3,1,2,0:T(8,128)(2,1)}, u32[]{:S(2)}, u32[]{:S(2)}) %all-to-all-start) | async-done | bytes 8388640 | tf_op jit(solution)/shard_map/all_to_all | solution.py:16
  261.0 9.8 copy.121
  270.8 16.2 %fusion.7 = (bf16[8,2,128,16,128]{4,2,3,0,1:T(8,128)(2,1)}, f32[2,128,8,16,128,1]{4,1,5,3,2,0:T(8,128)}) fusion(f32[8,128,16]{1,2,0:T(8,128)S(1)} %convert_element_type.129, bf16[8,2,128,16,128]{4,3,2,1,0:T(8,128)(2,1)} %param.4, bf16[8,2,128,16,128]{4,3,2,1,0:T(8,128)(2,1)} %bitcast.331, bf16[1,2,128,128]{2,3,0,1:T(8,128)(2,1)S(1)} %get-tuple-element.28, ...), kind=kOutput, calls=%fused_computation.33 | convolution fusion | flops 2168717312 | bytes 42139648 | tf_op jit(solution)/shard_map/ckzyx,kjzw->cjwyx/dot_general | solution.py:59
  287.0 8.0 fusion.9
  295.0 12.0 %copy.126 = bf16[8,2,128,16,128]{4,3,0,1,2:T(8,128)(2,1)} copy(bf16[8,2,128,16,128]{4,2,3,0,1:T(8,128)(2,1)} %fusion.9) | data formatting | bytes 16777216 | tf_op jit(solution)/shard_map/convert_element_type | solution.py:74
  307.0 189.2 %all_to_all.46 = bf16[8,2,128,16,128]{4,3,0,1,2:T(8,128)(2,1)} all-to-all(bf16[8,2,128,16,128]{4,3,0,1,2:T(8,128)(2,1)} %copy.126), channel_id=1, replica_groups=mesh['coil'=4,'slab'=8] {'slab'}, dimensions={2} | all-to-all | bytes 16777216 | tf_op jit(solution)/shard_map/all_to_all | solution.py:77
  496.2 9.1 copy.128
  505.3 10.3 convolution_bitcast_fusion.1
  515.6 11.3 fusion.17
  556.6 9.4 reduce-scatter.3.cloned.1.call-done
  569.5 22.7 %all-gather.5.cloned.1.call-done = f32[2,16,128,128]{3,1,0,2:T(8,128)} async-done(((f32[2,16,32,128]{3,1,0,2:T(8,128)}), f32[2,16,128,128]{3,1,0,2:T(8,128)}) %all-gather.5.cloned.1.call-update) | async-done | bytes 2097168 | tf_op jit(solution)/shard_map/all_gather | solution.py:135
  594.5 8.1 fusion.21
  602.6 9.0 fusion.10
  624.0 189.0 %all_to_all.47 = bf16[8,8,2,16,16,128]{5,4,3,1,2,0:T(8,128)(2,1)} all-to-all(bf16[8,8,2,16,16,128]{5,4,3,1,2,0:T(8,128)(2,1)S(1)} %fusion.76), channel_id=1, replica_groups=mesh['coil'=4,'slab'=8] {'slab'}, dimensions={0} | all-to-all | bytes 16777216 | tf_op jit(solution)/shard_map/all_to_all | solution.py:16
  813.1 9.8 copy.141
  822.8 21.0 %fusion.6 = bf16[8,2,128,16,128]{4,2,3,0,1:T(8,128)(2,1)} fusion(f32[2,128,8,16,128,1]{4,1,5,3,2,0:T(8,128)} %get-tuple-element.34, f32[8,128,16]{1,2,0:T(8,128)S(1)} %convert_element_type.129, bf16[8,2,128,16,128]{4,3,2,1,0:T(8,128)(2,1)} %param.4, bf16[8,2,128,16,128]{4,3,2,1,0:T(8,128)(2,1)} %bitcast.340, ...), kind=kOutput, calls=%fused_computation.24 | convolution fusion | flops 2189688832 | bytes 42139648 | tf_op jit(solution)/shard_map/ckzyx,kjzw->cjwyx/dot_general | solution.py:59
  851.8 12.0 %copy.145 = bf16[8,2,128,16,128]{4,3,0,1,2:T(8,128)(2,1)} copy(bf16[8,2,128,16,128]{4,2,3,0,1:T(8,128)(2,1)} %fusion.11) | data formatting | bytes 16777216 | tf_op jit(solution)/shard_map/convert_element_type | solution.py:74
  863.8 188.7 %all_to_all.48 = bf16[8,2,128,16,128]{4,3,0,1,2:T(8,128)(2,1)} all-to-all(bf16[8,2,128,16,128]{4,3,0,1,2:T(8,128)(2,1)} %copy.145), channel_id=1, replica_groups=mesh['coil'=4,'slab'=8] {'slab'}, dimensions={2} | all-to-all | bytes 16777216 | tf_op jit(solution)/shard_map/all_to_all | solution.py:77
  1052.5 9.1 copy.147
  1061.7 10.3 convolution_bitcast_fusion
  1071.9 11.3 fusion.25
  1111.8 10.5 reduce-scatter.5.cloned.1.call-done
  (101 shorter events, 124.3 us)
Async XLA Ops:
  6.5 27.7 %all-gather.3.cloned.1.call-start = ((), (), s32[]{:S(2)}) async-start(), calls=%async_computation.6 | async-start | bytes 2621440 | tf_op jit(solution)/shard_map/all_gather | solution.py:135
  34.2 4.0 copy-start.1
  71.8 5.7 copy-start.10
  71.8 189.2 %all-to-all-start = ((bf16[8,8,2,16,16,128]{5,4,3,1,2,0:T(8,128)(2,1)}), bf16[8,8,2,16,16,128]{5,4,3,1,2,0:T(8,128)(2,1)}, u32[]{:S(2)}, u32[]{:S(2)}) async-start(bf16[8,8,2,16,16,128]{5,4,3,1,2,0:T(8,128)(2,1)} %fusion.84), calls=%async_computation | async-start | bytes 16777216 | tf_op jit(solution)/shard_map/all_to_all | solution.py:16
  77.5 488.6 %reduce-scatter.3.cloned.1.call-start = ((), (), s32[]{:S(2)}) async-start(), calls=%async_computation.7 | async-start | bytes 2621440 | tf_op jit(solution)/shard_map/reduce_scatter | solution.py:145
  526.9 10.2 copy-start
  537.1 55.1 %all-gather.5.cloned.1.call-start = ((), (), s32[]{:S(2)}) async-start(), calls=%async_computation.8 | async-start | bytes 2621440 | tf_op jit(solution)/shard_map/all_gather | solution.py:135
  537.2 6.9 collective-permute-start
  545.4 20.7 %copy-start.9 = (f32[2,16,32,128]{3,2,1,0:T(8,128)S(1)}, f32[2,16,32,128]{3,2,1,0:T(8,128)}, u32[]{:S(2)}) copy-start(f32[2,16,32,128]{3,2,1,0:T(8,128)} %param.7) | copy-start | bytes 1572868
  548.7 1.3 copy-start.5
  550.2 6.4 collective-permute-start.1
  569.4 552.9 %reduce-scatter.5.cloned.1.call-start = ((), (), s32[]{:S(2)}) async-start(), calls=%async_computation.9 | async-start | bytes 2621440 | tf_op jit(solution)/shard_map/reduce_scatter | solution.py:145
  1083.2 10.1 copy-start.2
  1093.4 2.7 copy-start.3
  1093.5 7.0 collective-permute-start.2
  1095.5 1.9 copy-start.4
  1096.1 4.4 copy-start.6
  1101.9 20.4 %copy-start.8 = (f32[2,16,32,128]{3,1,0,2:T(8,128)S(1)}, f32[2,16,32,128]{3,1,0,2:T(8,128)}, u32[]{:S(2)}) copy-start(f32[2,16,32,128]{3,1,0,2:T(8,128)} %get-tuple-element.12) | copy-start | bytes 1572868
  1104.7 4.6 copy-start.7
  1104.8 6.9 collective-permute-start.3
Sparse Core Ops, SparseCore 0:
  8.9 25.2 all-gather.2
  537.2 28.8 reduce-scatter.2
  569.5 22.5 all-gather.4
  1093.5 28.7 reduce-scatter.4
